TPU v7x, 32 devices: a whole 2x2x4 slice. The times are simulated.
32 devices in a mesh: gx: 4 (over z), gy: 4 (over y, x), gz: 2 (over core).
Axes of the slice: x: 2, y: 2, z: 4, core: 2. Of those that a mesh axis runs over, the one named last changes fastest.
Arguments:
- panel: float32 [8192, 4096], P(('gx', 'gy', 'gz'))
- treat_start: int32 [8192], P(('gx', 'gy', 'gz')), may hold values from 1024 to 4096
- loading_init: float32 [64, 8192], P(None, ('gx', 'gy', 'gz'))
- factor_init: float32 [64, 4096], P(None, ('gx', 'gy', 'gz'))
- unit_init: float32 [8192], P(('gx', 'gy', 'gz'))
- day_init: float32 [4096], replicated
Outputs:
- loading_out: float32 [64, 8192], P(None, ('gx', 'gy', 'gz'))
- factor_out: float32 [64, 4096], P(None, ('gx', 'gy', 'gz'))
- unit_out: float32 [8192], P(('gx', 'gy', 'gz'))
- day_out: float32 [4096], replicated
Inputs may be any that keep to these rules, and one draw needn't show every extreme that they name: A unit is treated from day treat_start on; 4096 means never treated.
All inputs are finite; a program needn't handle non-finite values.
Results may differ from a plain program's by a relative error of at most 0.0001.
Values sent between devices are 32-bit elements; how exact they have to be, the bound alone decides.
A program may use at most 64 MiB of HBM per device.

v0:
```python
import jax
import jax.numpy as jnp
from jax import lax
from jax.sharding import PartitionSpec as P

SWEEPS = 2
RIDGE = 1.0


def solve_spd(matrix, right):
    lower = jnp.linalg.cholesky(matrix)
    middle = lax.linalg.triangular_solve(lower, right, left_side=True, lower=True)
    return lax.linalg.triangular_solve(lower, middle, left_side=True, lower=True, transpose_a=True)


def contract_first(left, right):
    return lax.dot_general(
        left,
        right,
        (((0,), (0,)), ((), ())),
        precision=lax.Precision.HIGHEST,
        preferred_element_type=jnp.float32,
    )


def contract_last(left, right):
    return lax.dot_general(
        left,
        right,
        (((1,), (1,)), ((), ())),
        precision=lax.Precision.HIGHEST,
        preferred_element_type=jnp.float32,
    )


def body(panel, treat_start, loading_init, factor_init, unit_init, day_init):
    unit_rows, total_days = panel.shape
    devices = lax.axis_size(("gx", "gy", "gz"))
    all_units = unit_rows * devices
    slice_days = factor_init.shape[1]
    rank = loading_init.shape[0]
    ridge_eye = jnp.eye(rank, dtype=jnp.float32) * RIDGE
    observed = lax.broadcasted_iota(jnp.int32, (unit_rows, total_days), 1) < treat_start[:, None]
    loading = loading_init
    unit_eff = unit_init
    day_eff = day_init
    factors = None
    owned_factors = factor_init
    for sweep_index in range(SWEEPS):
        unit_gram = lax.psum(contract_last(loading, loading), ("gx", "gy", "gz"))
        if sweep_index == 0:
            fitted = contract_first(
                loading, lax.all_gather(factor_init, ("gx", "gy", "gz"), axis=1, tiled=True)
            )
        else:
            fitted = contract_first(loading, factors)
        imputed = jnp.where(observed, panel, unit_eff[:, None] + day_eff[None, :] + fitted)
        without = imputed - fitted
        day_part = jnp.sum(without, 0)
        row_sums = jnp.sum(without, 1)
        resid = None
        day_sums = lax.psum(day_part, ("gx", "gy", "gz"))
        grand = jnp.sum(day_sums) / (all_units * total_days)
        day_eff = day_sums / all_units - grand
        unit_eff = row_sums / total_days - grand
        resid = imputed - unit_eff[:, None] - day_eff[None, :]
        payload = jnp.dot(loading, resid, precision=lax.Precision.HIGHEST)
        summed = lax.psum(payload, ("gx", "gy", "gz"))
        factors = solve_spd(unit_gram + ridge_eye, summed)
        owned_factors = lax.dynamic_slice_in_dim(
            factors, lax.axis_index(("gx", "gy", "gz")) * slice_days, slice_days, 1
        )
        factor_gram = jnp.dot(factors, factors.T, precision=lax.Precision.HIGHEST)
        loading = solve_spd(factor_gram + ridge_eye, contract_last(factors, resid))
    return (loading, owned_factors, unit_eff, day_eff)


def solution(mesh):
    return jax.shard_map(
        body,
        mesh=mesh,
        in_specs=(
            P(("gx", "gy", "gz"), None),
            P(("gx", "gy", "gz")),
            P(None, ("gx", "gy", "gz")),
            P(None, ("gx", "gy", "gz")),
            P(("gx", "gy", "gz")),
            P(),
        ),
        out_specs=(
            P(None, ("gx", "gy", "gz")),
            P(None, ("gx", "gy", "gz")),
            P(("gx", "gy", "gz")),
            P(),
        ),
        check_vma=False,
    )
```

profile of v0, /device:TPU:0, one launch (start us, length us, event | category | flops | bytes accessed | tf_op | source)
XLA Modules:
  0.0 507.0 jit_solution(17631101533937465551)
XLA Ops:
  7.2 0.7 all-gather.2.cloned.1.call-update
  8.0 0.2 fusion.41
  8.3 57.7 %all-gather.2.cloned.1.call-done = f32[64,4096]{1,0:T(8,128)} async-done(((f32[64,128]{1,0:T(8,128)}), f32[64,4096]{1,0:T(8,128)}) %all-gather.2.cloned.1.call-update) | async-done | bytes 1048592 | tf_op jit(solution)/shard_map/all_gather | solution.py:53
  65.9 7.9 %subtract_reduce_fusion.3 = (f32[256]{0:T(256)S(1)}, f32[4096]{0:T(1024)S(1)}, f32[256,4096]{1,0:T(8,128)}) fusion(f32[256,4096]{1,0:T(8,128)} %param.15, f32[4096]{0:T(1024)} %param.20, f32[256]{0:T(256)} %param.19, s32[256]{0:T(256)} %param.16, f32[64,256]{1,0:T(8,128)S(1)} %copy-done, f32[64,4096]{1,0:T(8,128)} %all-gather.2.cloned.1.call-done), kind=kOutput, calls=%fused_computation.20 | convolution fusion | flops 812642048 | bytes 9538560 | tf_op jit(solution)/shard_map/dot_general | solution.py:17
  73.8 40.5 %all-reduce.1 = (f32[4096]{0:T(1024)S(1)}, f32[64,64]{0,1:T(8,128)S(1)}) all-reduce(f32[4096]{0:T(1024)S(1)} %get-tuple-element.12, f32[64,64]{0,1:T(8,128)S(1)} %fusion.41), channel_id=1, replica_groups=mesh['gx'=4,'gy'=4,'gz'=2] {'gx','gy','gz'}, use_global_device_ids=true, to_apply=%region_5.0 | all-reduce | flops 8192 | bytes 65536 | tf_op jit(solution)/shard_map/psum | solution.py:62
  114.3 0.6 reduce_sum.56
  115.6 12.0 %convolution_bitcast_fusion = f32[64,4096]{0,1:T(8,128)} fusion(f32[64,256]{1,0:T(8,128)S(1)} %copy-done, f32[4096]{0:T(1024)S(1)} %multiply_subtract_fusion.1, f32[256]{0:T(256)S(1)} %multiply_subtract_fusion.3, f32[256,4096]{1,0:T(8,128)} %param.15, f32[256,4096]{1,0:T(8,128)} %get-tuple-element.17, f32[4096]{0:T(1024)S(1)} %copy-done.3, ...), kind=kOutput, calls=%fused_computation | convolution fusion | flops 811597824 | bytes 9538560 | tf_op jit(solution)/shard_map/dot_general | solution.py:67
  127.6 10.1 %all-reduce.7.cloned.1.call-start = ((), (), s32[]{:S(2)}) async-start(), calls=%async_computation.2 | async-start | bytes 2097152 | tf_op jit(solution)/shard_map/psum | solution.py:68
  137.7 0.1 copy.11
  137.8 5.8 %cholesky.74 = f32[64,64]{1,0:T(8,128)S(1)} custom-call(f32[64,64]{1,0:T(8,128)S(1)} %fusion.34), custom_call_target="Cholesky" | custom-call | tf_op jit(solution)/shard_map/jit(cholesky)/cholesky | solution.py:11
  143.7 0.6 compare_reduce_fusion.3
  144.3 0.7 fusion.11
  145.0 4.9 custom-call.19
  149.9 111.7 %all-reduce.5.cloned.1.call-done = f32[64,4096]{0,1:T(8,128)} async-done(((f32[64,4096]{0,1:T(8,128)}), f32[64,4096]{0,1:T(8,128)}) %all-reduce.5.cloned.1.call-update) | async-done | bytes 1048592 | tf_op jit(solution)/shard_map/psum | solution.py:68
  261.6 4.1 fusion.30
  265.7 1.0 fusion.32
  266.7 1.0 convolution_add_fusion.1
  267.7 6.6 %fusion = f32[64,256]{1,0:T(8,128)S(1)} fusion(f32[64,4096]{1,0:T(8,128)S(1)} %fusion.32, f32[4096]{0:T(1024)S(1)} %multiply_subtract_fusion.1, f32[256]{0:T(256)S(1)} %multiply_subtract_fusion.3, f32[256,4096]{1,0:T(8,128)S(1)} %copy-done.1, f32[256,4096]{1,0:T(8,128)} %get-tuple-element.17, f32[4096]{0:T(1024)S(1)} %copy-done.3, f32[256]{0:T(256)S(1)} %copy-done.6, ...), kind=kOutput, calls=%fused_computation.6 | convolution fusion | flops 811597824 | bytes 9538560 | tf_op jit(solution)/shard_map/dot_general | solution.py:27
  274.3 0.1 copy.13
  274.4 5.8 %cholesky.85 = f32[64,64]{1,0:T(8,128)S(1)} custom-call(f32[64,64]{1,0:T(8,128)S(1)} %fusion.29), custom_call_target="Cholesky" | custom-call | tf_op jit(solution)/shard_map/jit(cholesky)/cholesky | solution.py:11
  280.3 0.6 compare_reduce_fusion.2
  281.0 0.7 fusion.12
  281.6 4.9 custom-call.21
  286.5 0.3 fusion.25
  286.8 0.2 fusion.27
  287.0 7.7 %subtract_reduce_fusion.1 = (f32[256]{0:T(256)S(1)}, f32[4096]{0:T(1024)S(1)}, f32[256,4096]{1,0:T(8,128)}) fusion(f32[256,4096]{1,0:T(8,128)} %param.15, f32[4096]{0:T(1024)S(1)} %multiply_subtract_fusion.1, f32[256]{0:T(256)S(1)} %multiply_subtract_fusion.3, s32[256]{0:T(256)S(1)} %copy-done.5, f32[64,256]{1,0:T(8,128)S(1)} %fusion.27, ...), kind=kOutput, calls=%fused_computation.18 | convolution fusion | flops 812642048 | bytes 9538560 | tf_op jit(solution)/shard_map/dot_general | solution.py:17
  294.7 0.2 fusion.42
  294.9 39.5 %all-reduce = (f32[4096]{0:T(1024)S(1)}, f32[64,64]{0,1:T(8,128)S(1)}) all-reduce(f32[4096]{0:T(1024)S(1)} %get-tuple-element.10, f32[64,64]{0,1:T(8,128)S(1)} %fusion.42), channel_id=1, replica_groups=mesh['gx'=4,'gy'=4,'gz'=2] {'gx','gy','gz'}, use_global_device_ids=true, to_apply=%region_11.17 | all-reduce | flops 8192 | bytes 65536 | tf_op jit(solution)/shard_map/psum | solution.py:62
  334.5 0.1 copy.15
  334.6 0.6 reduce_sum.59
  335.9 8.1 %fusion.2 = f32[64,4096]{1,0:T(8,128)} fusion(f32[64,256]{1,0:T(8,128)S(1)} %fusion.27, f32[4096]{0:T(1024)S(1)} %multiply_subtract_fusion, f32[256]{0:T(256)S(1)} %multiply_subtract_fusion.2, f32[256,4096]{1,0:T(8,128)} %param.15, f32[256,4096]{1,0:T(8,128)} %get-tuple-element.18, f32[4096]{0:T(1024)S(1)} %multiply_subtract_fusion.1, ...), kind=kOutput, calls=%fused_computation.8 | convolution fusion | flops 811597824 | bytes 9538560 | tf_op jit(solution)/shard_map/dot_general | solution.py:67
  344.0 5.8 %cholesky.96 = f32[64,64]{1,0:T(8,128)S(1)} custom-call(f32[64,64]{1,0:T(8,128)S(1)} %fusion.24), custom_call_target="Cholesky" | custom-call | tf_op jit(solution)/shard_map/jit(cholesky)/cholesky | solution.py:11
  349.9 0.6 compare_reduce_fusion.1
  350.5 0.7 fusion.13
  351.2 4.9 custom-call.23
  356.1 119.0 %all-reduce.7.cloned.1.call-done = f32[64,4096]{1,0:T(8,128)} async-done(((f32[64,4096]{1,0:T(8,128)}), f32[64,4096]{1,0:T(8,128)}) %all-reduce.7.cloned.1.call-update) | async-done | bytes 1048592 | tf_op jit(solution)/shard_map/psum | solution.py:68
  475.1 2.4 fusion.20
  477.5 1.0 fusion.22
  478.5 1.0 convolution_add_fusion
  479.5 6.6 %fusion.1 = f32[64,256]{1,0:T(8,128)S(1)} fusion(f32[64,4096]{1,0:T(8,128)S(1)} %fusion.22, f32[4096]{0:T(1024)S(1)} %multiply_subtract_fusion, f32[256]{0:T(256)S(1)} %multiply_subtract_fusion.2, f32[256,4096]{1,0:T(8,128)S(1)} %copy-done.2, f32[256,4096]{1,0:T(8,128)} %get-tuple-element.18, f32[4096]{0:T(1024)S(1)} %multiply_subtract_fusion.1, ...), kind=kOutput, calls=%fused_computation.7 | convolution fusion | flops 811597824 | bytes 9538560 | tf_op jit(solution)/shard_map/dot_general | solution.py:27
  486.2 0.1 copy.17
  486.2 5.8 %cholesky.107 = f32[64,64]{1,0:T(8,128)S(1)} custom-call(f32[64,64]{1,0:T(8,128)S(1)} %fusion.19), custom_call_target="Cholesky" | custom-call | tf_op jit(solution)/shard_map/jit(cholesky)/cholesky | solution.py:11
  492.1 0.6 compare_reduce_fusion
  492.8 0.7 fusion.14
  493.4 4.9 custom-call.25
  498.3 0.3 fusion.15
  498.6 0.8 fusion.17
  499.4 0.6 constant_dynamic-slice_fusion
  (34 shorter events, 0.4 us)
Async XLA Ops:
  7.2 0.8 copy-start
  7.2 58.7 %all-gather.2.cloned.1.call-start = ((), (), s32[]{:S(2)}) async-start(), calls=%async_computation | async-start | bytes 1081344 | tf_op jit(solution)/shard_map/all_gather | solution.py:53
  7.9 253.7 %all-reduce.5.cloned.1.call-start = ((), (), s32[]{:S(2)}) async-start(), calls=%async_computation.1 | async-start | bytes 4194304 | tf_op jit(solution)/shard_map/psum | solution.py:68
  8.2 107.4 %copy-start.3 = (f32[4096]{0:T(1024)S(1)}, f32[4096]{0:T(1024)}, u32[]{:S(2)}) copy-start(f32[4096]{0:T(1024)} %param.20) | copy-start | bytes 49156
  8.2 107.4 %copy-start.5 = (s32[256]{0:T(256)S(1)}, s32[256]{0:T(256)}, u32[]{:S(2)}) copy-start(s32[256]{0:T(256)} %param.16) | copy-start | bytes 3076
  8.2 107.4 %copy-start.6 = (f32[256]{0:T(256)S(1)}, f32[256]{0:T(256)}, u32[]{:S(2)}) copy-start(f32[256]{0:T(256)} %param.19) | copy-start | bytes 3076
  127.6 347.5 %all-reduce.7.cloned.1.call-start = ((), (), s32[]{:S(2)}) async-start(), calls=%async_computation.2 | async-start | bytes 2097152 | tf_op jit(solution)/shard_map/psum | solution.py:68
  261.6 6.1 %copy-start.1 = (f32[256,4096]{1,0:T(8,128)S(1)}, f32[256,4096]{1,0:T(8,128)}, u32[]{:S(2)}) copy-start(f32[256,4096]{1,0:T(8,128)} %param.15) | copy-start | bytes 12582916
  335.8 143.6 %copy-start.4 = (f32[4096]{0:T(1024)}, f32[4096]{0:T(1024)S(1)}, u32[]{:S(2)}) copy-start(f32[4096]{0:T(1024)S(1)} %multiply_subtract_fusion) | copy-start | bytes 49156
  335.9 143.6 %copy-start.7 = (f32[256]{0:T(256)}, f32[256]{0:T(256)S(1)}, u32[]{:S(2)}) copy-start(f32[256]{0:T(256)S(1)} %multiply_subtract_fusion.2) | copy-start | bytes 3076
  475.1 4.4 copy-start.2
Sparse Core Ops, SparseCore 0:
  10.9 55.0 all-gather.1
  127.7 133.8 all-reduce.4
  344.1 130.8 all-reduce.6
where the time goes:
time: 515 us; the launch traced here: 507 us
  waiting for transfers between devices  289 us (56%)
  blocking collectives  80 us (16%)
  matrix products  61.4 us (12%)
  other arithmetic  49.6 us (10%)
  between operations  15.8 us (3%)
  starting transfers between devices  10.2 us (2%)
    psum x2, waiting for transfers between devices, body(): summed = lax.psum(payload, ('gx', 'gy', 'gz'))  231 us
    psum x2, blocking collectives, body(): day_sums = lax.psum(day_part, ('gx', 'gy', 'gz'))  80 us
    all_gather x1, waiting for transfers between devices, body(): lax.all_gather(factor_init, ('gx', 'gy', 'gz'), axis=1, tiled=True)  57.7 us
    another operation x12, other arithmetic, solve_spd(): lower = jnp.linalg.cholesky(matrix)  26.1 us
    another operation x8, other arithmetic, solve_spd(): lax.linalg.triangular_solve(lower, middle, left_side=True, lower=True, tr...  22.2 us
    dot_general x2, matrix products, body(): payload = jnp.dot(loading, resid, precision=lax.Precision.HIGHEST)  20 us
    dot_general x2, matrix products, contract_first(): lax.dot_general(left, right, (((0,), (0,)), ((), ())), precision=lax.Prec...  15.6 us
    dot_general x4, matrix products, contract_last(): lax.dot_general(left, right, (((1,), (1,)), ((), ())), precision=lax.Prec...  13.7 us
  transfers between devices with their start and end apart: 3, of which 3 were waited for; matrix products, arithmetic and copies ran while one was open for 5% of the time, Pallas kernels for 0%

commit v1 on v0

--- a/solution.py
+++ b/solution.py
@@ -65,7 +65,7 @@
         unit_eff = row_sums / total_days - grand
         resid = imputed - unit_eff[:, None] - day_eff[None, :]
         payload = jnp.dot(loading, resid, precision=lax.Precision.HIGHEST)
-        summed = lax.psum(payload, ("gx", "gy", "gz"))
+        summed = jnp.sum(lax.all_gather(payload, ("gx", "gy", "gz")), axis=0)
         factors = solve_spd(unit_gram + ridge_eye, summed)
         owned_factors = lax.dynamic_slice_in_dim(
             factors, lax.axis_index(("gx", "gy", "gz")) * slice_days, slice_days, 1

time: 515 us -> 646 us (1.25); the launches traced: 507 us -> 645 us
  waiting for transfers between devices: 289 us -> 423 us
  other arithmetic: 49.6 us -> 73.3 us
  starting transfers between devices: 10.2 us -> 0.12 us
  matrix products: 61.4 us -> 53.2 us
    all_gather x0 -> x2, waiting for transfers between devices: none -> 364 us  [body(): summed = jnp.sum(lax.all_gather(payload, ('gx', 'gy', 'gz')), axis=0)]
    psum x2 -> x0, waiting for transfers between devices: 231 us -> none  [body(): summed = lax.psum(payload, ('gx', 'gy', 'gz'))]
    reduce_sum x0 -> x2, other arithmetic: none -> 23.7 us  [body(): summed = jnp.sum(lax.all_gather(payload, ('gx', 'gy', 'gz')), axis=0)]
    psum x2 -> x0, starting transfers between devices: 10.1 us -> none  [body(): summed = lax.psum(payload, ('gx', 'gy', 'gz'))]
  transfers between devices with their start and end apart: 3 -> 3, of which waited for: 3 -> 3; matrix products, arithmetic and copies ran while one was open for 5% -> 4% of each run, Pallas kernels for 0% -> 0%
where the time goes in v1:
time: 646 us; the launch traced here: 645 us
  waiting for transfers between devices  423 us (65%)
  blocking collectives  79.4 us (12%)
  other arithmetic  73.3 us (11%)
  matrix products  53.2 us (8%)
  between operations  15.4 us (2%)
    all_gather x2, waiting for transfers between devices, body(): summed = jnp.sum(lax.all_gather(payload, ('gx', 'gy', 'gz')), axis=0)  364 us
    psum x2, blocking collectives, body(): day_sums = lax.psum(day_part, ('gx', 'gy', 'gz'))  79.4 us
    all_gather x1, waiting for transfers between devices, body(): lax.all_gather(factor_init, ('gx', 'gy', 'gz'), axis=1, tiled=True)  57.7 us
    another operation x12, other arithmetic, solve_spd(): lower = jnp.linalg.cholesky(matrix)  26.1 us
    reduce_sum x2, other arithmetic, body(): summed = jnp.sum(lax.all_gather(payload, ('gx', 'gy', 'gz')), axis=0)  23.7 us
    another operation x8, other arithmetic, solve_spd(): lax.linalg.triangular_solve(lower, middle, left_side=True, lower=True, tr...  22.2 us
    dot_general x2, matrix products, body(): payload = jnp.dot(loading, resid, precision=lax.Precision.HIGHEST)  16.2 us
    dot_general x2, matrix products, contract_first(): lax.dot_general(left, right, (((0,), (0,)), ((), ())), precision=lax.Prec...  15.7 us
  transfers between devices with their start and end apart: 3, of which 3 were waited for; matrix products, arithmetic and copies ran while one was open for 4% of the time, Pallas kernels for 0%

profile of v1, /device:TPU:0, one launch (start us, length us, event | category | flops | bytes accessed | tf_op | source)
XLA Modules:
  0.0 645.1 jit_solution(2071144809108555544)
XLA Ops:
  7.2 0.7 all-gather.6.cloned.1.call-update
  8.0 0.2 fusion.41
  8.3 57.7 %all-gather.6.cloned.1.call-done = f32[64,4096]{1,0:T(8,128)} async-done(((f32[64,128]{1,0:T(8,128)}), f32[64,4096]{1,0:T(8,128)}) %all-gather.6.cloned.1.call-update) | async-done | bytes 1048592 | tf_op jit(solution)/shard_map/all_gather | solution.py:53
  65.9 8.0 %subtract_reduce_fusion.3 = (f32[256]{0:T(256)S(1)}, f32[4096]{0:T(1024)S(1)}, f32[256,4096]{1,0:T(8,128)}) fusion(f32[256,4096]{1,0:T(8,128)} %param.15, f32[4096]{0:T(1024)} %param.20, f32[256]{0:T(256)} %param.19, s32[256]{0:T(256)} %param.16, f32[64,256]{1,0:T(8,128)S(1)} %copy-done, f32[64,4096]{1,0:T(8,128)} %all-gather.6.cloned.1.call-done), kind=kOutput, calls=%fused_computation.20 | convolution fusion | flops 812642048 | bytes 9538560 | tf_op jit(solution)/shard_map/dot_general | solution.py:17
  73.9 40.4 %all-reduce.1 = (f32[4096]{0:T(1024)S(1)}, f32[64,64]{0,1:T(8,128)S(1)}) all-reduce(f32[4096]{0:T(1024)S(1)} %get-tuple-element.12, f32[64,64]{0,1:T(8,128)S(1)} %fusion.41), channel_id=1, replica_groups=mesh['gx'=4,'gy'=4,'gz'=2] {'gx','gy','gz'}, use_global_device_ids=true, to_apply=%region_5.0 | all-reduce | flops 8192 | bytes 65536 | tf_op jit(solution)/shard_map/psum | solution.py:62
  114.3 0.6 reduce_sum.74
  115.7 8.2 %convolution_bitcast_fusion = f32[64,4096]{1,0:T(8,128)} fusion(f32[64,256]{1,0:T(8,128)S(1)} %copy-done, f32[4096]{0:T(1024)S(1)} %multiply_subtract_fusion.1, f32[256]{0:T(256)S(1)} %multiply_subtract_fusion.3, f32[256,4096]{1,0:T(8,128)} %param.15, f32[256,4096]{1,0:T(8,128)} %get-tuple-element.17, f32[4096]{0:T(1024)S(1)} %copy-done.4, ...), kind=kOutput, calls=%fused_computation | convolution fusion | flops 811597824 | bytes 9538560 | tf_op jit(solution)/shard_map/dot_general | solution.py:67
  124.0 0.1 copy.11
  124.1 5.8 cholesky.74
  129.9 0.6 compare_reduce_fusion.3
  130.6 0.7 fusion.11
  131.3 4.9 custom-call.19
  136.1 181.2 %all-gather.8.cloned.1.call-done = f32[2048,4096]{1,0:T(8,128)} async-done(((f32[64,4096]{1,0:T(8,128)}), f32[2048,4096]{1,0:T(8,128)}) %all-gather.8.cloned.1.call-update) | async-done | bytes 33554448 | tf_op jit(solution)/shard_map/all_gather | solution.py:68
  317.4 11.8 %reduce_sum.75 = f32[64,4096]{1,0:T(8,128)S(1)} reduce(f32[32,64,4096]{2,1,0:T(8,128)} %bitcast.81, f32[]{:T(128)} %constant.62.clone.1), dimensions={0}, to_apply=%region_7.9 | reduce | flops 8126464 | bytes 34603012 | tf_op jit(solution)/shard_map/reduce_sum | solution.py:68
  329.2 1.0 fusion.30
  330.3 1.0 fusion.32
  331.3 1.0 convolution_add_fusion.1
  332.3 6.6 %fusion = f32[64,256]{1,0:T(8,128)S(1)} fusion(f32[64,4096]{1,0:T(8,128)S(1)} %fusion.32, f32[4096]{0:T(1024)S(1)} %multiply_subtract_fusion.1, f32[256]{0:T(256)S(1)} %multiply_subtract_fusion.3, f32[256,4096]{1,0:T(8,128)S(1)} %copy-done.2, f32[256,4096]{1,0:T(8,128)} %get-tuple-element.17, f32[4096]{0:T(1024)S(1)} %copy-done.4, f32[256]{0:T(256)S(1)} %copy-done.7, ...), kind=kOutput, calls=%fused_computation.6 | convolution fusion | flops 811597824 | bytes 9538560 | tf_op jit(solution)/shard_map/dot_general | solution.py:27
  339.0 0.1 copy.13
  339.1 5.8 cholesky.85
  344.9 0.6 compare_reduce_fusion.2
  345.6 0.7 fusion.12
  346.2 4.9 custom-call.21
  351.1 0.3 fusion.25
  351.4 0.2 fusion.27
  351.6 7.7 %subtract_reduce_fusion.1 = (f32[256]{0:T(256)S(1)}, f32[4096]{0:T(1024)S(1)}, f32[256,4096]{1,0:T(8,128)}) fusion(f32[256,4096]{1,0:T(8,128)} %param.15, f32[4096]{0:T(1024)S(1)} %multiply_subtract_fusion.1, f32[256]{0:T(256)S(1)} %multiply_subtract_fusion.3, s32[256]{0:T(256)S(1)} %copy-done.6, f32[64,256]{1,0:T(8,128)S(1)} %fusion.27, ...), kind=kOutput, calls=%fused_computation.18 | convolution fusion | flops 812642048 | bytes 9538560 | tf_op jit(solution)/shard_map/dot_general | solution.py:17
  359.3 0.2 fusion.42
  359.5 39.0 %all-reduce = (f32[4096]{0:T(1024)S(1)}, f32[64,64]{0,1:T(8,128)S(1)}) all-reduce(f32[4096]{0:T(1024)S(1)} %get-tuple-element.10, f32[64,64]{0,1:T(8,128)S(1)} %fusion.42), channel_id=1, replica_groups=mesh['gx'=4,'gy'=4,'gz'=2] {'gx','gy','gz'}, use_global_device_ids=true, to_apply=%region_11.17 | all-reduce | flops 8192 | bytes 65536 | tf_op jit(solution)/shard_map/psum | solution.py:62
  398.5 0.6 reduce_sum.78
  399.8 8.0 %fusion.2 = f32[64,4096]{1,0:T(8,128)} fusion(f32[64,256]{1,0:T(8,128)S(1)} %fusion.27, f32[4096]{0:T(1024)S(1)} %multiply_subtract_fusion, f32[256]{0:T(256)S(1)} %multiply_subtract_fusion.2, f32[256,4096]{1,0:T(8,128)} %param.15, f32[256,4096]{1,0:T(8,128)} %get-tuple-element.18, f32[4096]{0:T(1024)S(1)} %multiply_subtract_fusion.1, ...), kind=kOutput, calls=%fused_computation.8 | convolution fusion | flops 811597824 | bytes 9538560 | tf_op jit(solution)/shard_map/dot_general | solution.py:67
  407.9 0.1 copy.15
  408.0 5.8 cholesky.96
  413.9 0.6 compare_reduce_fusion.1
  414.5 0.7 fusion.13
  415.2 4.9 custom-call.23
  420.1 182.9 %all-gather.10.cloned.1.call-done = f32[2048,4096]{1,0:T(8,128)} async-done(((f32[64,4096]{1,0:T(8,128)}), f32[2048,4096]{1,0:T(8,128)}) %all-gather.10.cloned.1.call-update) | async-done | bytes 33554448 | tf_op jit(solution)/shard_map/all_gather | solution.py:68
  603.0 11.9 %reduce_sum.79 = f32[64,4096]{1,0:T(8,128)S(1)} reduce(f32[32,64,4096]{2,1,0:T(8,128)} %bitcast.80, f32[]{:T(128)} %constant.62.clone.1), dimensions={0}, to_apply=%region_13.19 | reduce | flops 8126464 | bytes 34603012 | tf_op jit(solution)/shard_map/reduce_sum | solution.py:68
  614.9 1.0 fusion.20
  615.9 1.0 fusion.22
  617.0 1.0 convolution_add_fusion
  618.0 6.6 %fusion.1 = f32[64,256]{1,0:T(8,128)S(1)} fusion(f32[64,4096]{1,0:T(8,128)S(1)} %fusion.22, f32[4096]{0:T(1024)S(1)} %multiply_subtract_fusion, f32[256]{0:T(256)S(1)} %multiply_subtract_fusion.2, f32[256,4096]{1,0:T(8,128)S(1)} %copy-done.3, f32[256,4096]{1,0:T(8,128)} %get-tuple-element.18, f32[4096]{0:T(1024)S(1)} %multiply_subtract_fusion.1, ...), kind=kOutput, calls=%fused_computation.7 | convolution fusion | flops 811597824 | bytes 9538560 | tf_op jit(solution)/shard_map/dot_general | solution.py:27
  624.7 5.8 cholesky.107
  630.6 0.6 compare_reduce_fusion
  631.2 0.7 fusion.14
  631.9 4.9 custom-call.25
  636.8 0.3 fusion.15
  637.1 0.8 fusion.17
  637.9 0.6 constant_dynamic-slice_fusion
  (38 shorter events, 0.6 us)
Async XLA Ops:
  7.2 0.8 copy-start
  7.2 58.7 %all-gather.6.cloned.1.call-start = ((), (), s32[]{:S(2)}) async-start(), calls=%async_computation | async-start | bytes 1081344 | tf_op jit(solution)/shard_map/all_gather | solution.py:53
  7.9 309.5 %all-gather.8.cloned.1.call-start = ((), (), s32[]{:S(2)}) async-start(), calls=%async_computation.1 | async-start | bytes 34603008 | tf_op jit(solution)/shard_map/all_gather | solution.py:68
  8.2 107.4 %copy-start.4 = (f32[4096]{0:T(1024)S(1)}, f32[4096]{0:T(1024)}, u32[]{:S(2)}) copy-start(f32[4096]{0:T(1024)} %param.20) | copy-start | bytes 49156
  8.2 107.4 %copy-start.6 = (s32[256]{0:T(256)S(1)}, s32[256]{0:T(256)}, u32[]{:S(2)}) copy-start(s32[256]{0:T(256)} %param.16) | copy-start | bytes 3076
  8.2 107.4 %copy-start.7 = (f32[256]{0:T(256)S(1)}, f32[256]{0:T(256)}, u32[]{:S(2)}) copy-start(f32[256]{0:T(256)} %param.19) | copy-start | bytes 3076
  123.9 479.1 %all-gather.10.cloned.1.call-start = ((), (), s32[]{:S(2)}) async-start(), calls=%async_computation.2 | async-start | bytes 34603008 | tf_op jit(solution)/shard_map/all_gather | solution.py:68
  329.2 3.1 copy-start.2
  399.8 218.2 %copy-start.5 = (f32[4096]{0:T(1024)}, f32[4096]{0:T(1024)S(1)}, u32[]{:S(2)}) copy-start(f32[4096]{0:T(1024)S(1)} %multiply_subtract_fusion) | copy-start | bytes 49156
  399.8 218.2 %copy-start.8 = (f32[256]{0:T(256)}, f32[256]{0:T(256)S(1)}, u32[]{:S(2)}) copy-start(f32[256]{0:T(256)S(1)} %multiply_subtract_fusion.2) | copy-start | bytes 3076
  614.9 3.1 copy-start.3
  616.9 21.6 %copy-start.1 = (f32[64,256]{1,0:T(8,128)S(1)}, f32[64,256]{1,0:T(8,128)}, u32[]{:S(2)}) copy-start(f32[64,256]{1,0:T(8,128)} %param.17) | copy-start | bytes 196612
Sparse Core Ops, SparseCore 0:
  10.9 55.0 all-gather.5
  124.0 193.3 all-gather.7
  408.0 194.9 all-gather.9
